TPU v7x, 32 devices: a whole 2x2x4 slice. The times are simulated.
32 devices in a mesh: replica: 8 (over z, x), tensor: 4 (over y, core).
Axes of the slice: x: 2, y: 2, z: 4, core: 2. Of those that a mesh axis runs over, the one named last changes fastest.
Arguments:
- queries: bfloat16 [512, 8192], P('replica', 'tensor'), may hold values from -18 to 18
- kv_new: bfloat16 [512, 2, 1024], P('replica', None, 'tensor'), may hold values from -7.5 to 7.5
- pool: bfloat16 [192, 128, 2, 1024], P('replica', None, None, 'tensor'), may hold values from -240 to 240
- page_table: int32 [16, 12], P('replica'), may hold values from 0 to 191, as said below
- hist_len: int32 [16], P('replica'), may hold values from 769 to 1536
- o_weight: bfloat16 [8192, 8192], P('tensor'), may hold values from -0.125 to 0.125
Outputs:
- mixed: bfloat16 [512, 8192], P(('replica', 'tensor'))
Inputs may be any that keep to these rules, and one draw needn't show every extreme that they name: `page_table`: no two entries are equal. The owner of page id g is the replica group g // 24. Among the live pages (entry j of conversation c with j * 128 < hist_len[c]) of the conversations of one replica group, at most 3 have any one owner, and in every group some owner holds exactly 3 of them.
All inputs are finite; a program needn't handle non-finite values.
Results may differ from a plain program's by a relative error of at most 0.014.
Values may be sent and summed in bfloat16 or wider, within the bound.
A program may use at most 128 MiB of HBM per device.

v0:
```python
import math

import jax
import jax.numpy as jnp
from jax import lax
from jax.sharding import PartitionSpec as P

HD = 128
PAGE = 128
SLOT = 3


floor_value = -1e30


def attend_part(asked, keys, values, allowed):
    scores = jnp.einsum(
        "bnkgd,btkd->bnkgt", asked, keys, preferred_element_type=jnp.float32
    ) / math.sqrt(HD)
    peak = jnp.max(jnp.where(allowed, scores, floor_value), axis=-1)
    weights = jnp.where(allowed, jnp.exp(scores - peak[..., None]), 0.0).astype(jnp.bfloat16)
    amount = jnp.sum(weights.astype(jnp.float32), axis=-1)
    summed = jnp.einsum("bnkgt,btkd->bnkgd", weights, values, preferred_element_type=jnp.float32)
    return (peak, amount, summed)


def merge(first, second):
    peak = jnp.maximum(first[0], second[0])
    keep = jnp.exp(first[0] - peak)
    take = jnp.exp(second[0] - peak)
    return (
        peak,
        keep * first[1] + take * second[1],
        keep[..., None] * first[2] + take[..., None] * second[2],
    )


def block_stats(asked, pages, dialog_ids, slot_fill):
    dialogs = asked.shape[0]
    slots, page_len = (pages.shape[0], pages.shape[1])
    kv_count = asked.shape[2]
    keys = pages[:, :, 0].reshape(slots, page_len, kv_count, HD)
    values = pages[:, :, 1].reshape(slots, page_len, kv_count, HD)
    belongs = (dialog_ids[:, None] == jnp.arange(dialogs, dtype=jnp.int32)[None, :]) & (
        slot_fill > 0
    )[:, None]
    picker = (dialog_ids[:, None] == jnp.arange(dialogs, dtype=jnp.int32)[None, :]).astype(
        asked.dtype
    )
    chosen = jnp.einsum(
        "sd,dnkgh->snkgh", picker, asked, preferred_element_type=jnp.float32
    ).astype(asked.dtype)
    allowed = (jnp.arange(page_len, dtype=jnp.int32)[None, :] < slot_fill[:, None])[
        :, None, None, None, :
    ]
    peak, amount, summed = attend_part(chosen, keys, values, allowed)
    select = belongs[:, :, None, None, None]
    peaks = jnp.where(select, peak[:, None], floor_value)
    highest = jnp.max(peaks, axis=0)
    factor = jnp.where(select, jnp.exp(peaks - highest[None]), 0.0)
    total = jnp.einsum("sdnkg,snkg->dnkg", factor, amount, precision=lax.Precision.HIGHEST)
    weighted = jnp.einsum("sdnkg,snkgh->dnkgh", factor, summed, precision=lax.Precision.HIGHEST)
    return (highest, total, weighted)


def request_lists(page_table, hist_len, groups, pool_size):
    dialogs, entries = page_table.shape
    position = jnp.arange(entries, dtype=jnp.int32)
    fills = jnp.clip(hist_len[:, None] - position[None, :] * PAGE, 0, PAGE).reshape(-1)
    owners = (page_table // pool_size).reshape(-1)
    shelf = (page_table % pool_size).reshape(-1)
    dialog_of = jnp.repeat(jnp.arange(dialogs, dtype=jnp.int32), entries)
    hits = (owners[:, None] == jnp.arange(groups, dtype=jnp.int32)[None, :]) & (fills > 0)[:, None]
    ranks = jnp.cumsum(hits.astype(jnp.int32), axis=0) - 1
    places = hits.T[:, None, :] & (
        ranks.T[:, None, :] == jnp.arange(SLOT, dtype=jnp.int32)[None, :, None]
    )
    picked = places.astype(jnp.int32)
    wanted = jnp.sum(picked * shelf[None, None, :], axis=-1)
    dialog_ids = jnp.sum(picked * dialog_of[None, None, :], axis=-1)
    slot_fill = jnp.sum(picked * fills[None, None, :], axis=-1)
    return (wanted, dialog_ids, slot_fill)


def local(queries, kv_new, pool, page_table, hist_len, o_weight):
    groups = lax.axis_size("replica")
    pool_size = pool.shape[0]
    dialogs = page_table.shape[0]
    token_rows = queries.shape[0]
    new_len = token_rows // dialogs
    kv_width = kv_new.shape[2]
    kv_count = kv_width // HD
    per_group = queries.shape[1] // kv_width
    asked = queries.reshape(dialogs, new_len, kv_count, per_group, HD)
    fresh = kv_new.reshape(dialogs, new_len, 2, kv_count, HD)
    order = jnp.arange(new_len, dtype=jnp.int32)
    causal = (order[None, :] <= order[:, None])[None, :, None, None, :]
    state = attend_part(asked, fresh[:, :, 0], fresh[:, :, 1], causal)
    wanted, dialog_ids, slot_fill = request_lists(page_table, hist_len, groups, pool_size)
    shelf_ids = lax.all_to_all(wanted, "replica", split_axis=0, concat_axis=0, tiled=True)
    outgoing = pool[shelf_ids]
    arrived = lax.all_to_all(outgoing, "replica", split_axis=0, concat_axis=0, tiled=True)

    def absorb_pages(carry, items):
        pages, owner_dialogs, owner_fill = items
        return (merge(carry, block_stats(asked, pages, owner_dialogs, owner_fill)), None)

    state, _ = lax.scan(absorb_pages, state, (arrived, dialog_ids, slot_fill))
    attended = (
        (state[2] / state[1][..., None])
        .astype(jnp.bfloat16)
        .reshape(token_rows, kv_count * per_group * HD)
    )
    return lax.psum_scatter(
        jnp.dot(attended, o_weight, preferred_element_type=jnp.float32).astype(jnp.bfloat16),
        "tensor",
        scatter_dimension=0,
        tiled=True,
    )


def solution(mesh):
    in_specs = (
        P("replica", "tensor"),
        P("replica", None, "tensor"),
        P("replica", None, None, "tensor"),
        P("replica", None),
        P("replica"),
        P("tensor", None),
    )
    out_specs = P(("replica", "tensor"), None)
    return jax.shard_map(local, mesh=mesh, in_specs=in_specs, out_specs=out_specs, check_vma=False)
```

profile of v0, /device:TPU:31, one launch (start us, length us, event | category | flops | bytes accessed | tf_op | source)
XLA Modules:
  0.0 332.9 jit_solution(4688032555728466961)
XLA Ops:
  9.0 6.7 %all_to_all.17 = s32[8,1,3]{2,1,0:T(1,128)S(1)} all-to-all(s32[8,1,3]{2,1,0:T(1,128)S(1)} %copy.92), channel_id=1, replica_groups=mesh['replica'=8,'tensor'=4] {'replica'}, dimensions={0} | all-to-all | bytes 192 | tf_op jit(solution)/shard_map/all_to_all | solution.py:100
  16.0 8.0 %gather_fusion = bf16[24,128,2,256]{3,2,1,0:T(2,128)(2,1)} fusion(bf16[24,128,2,256]{3,2,1,0:T(2,128)(2,1)S(1)} %copy-done, s32[1024]{0:T(1024)S(1)} %pad_clamp_fusion), kind=kCustom, calls=%fused_computation | custom fusion | bytes 6291552 | tf_op jit(solution)/shard_map/gather | solution.py:101
  24.0 4.2 %copy.95 = bf16[24,128,2,256]{3,1,2,0:T(8,128)(2,1)} copy(bf16[24,128,2,256]{3,2,1,0:T(2,128)(2,1)} %gather_fusion) | data formatting | bytes 6291456 | tf_op jit(solution)/shard_map/gather | solution.py:101
  28.2 8.4 %all-to-all-start.1 = ((bf16[8,3,128,2,256]{4,2,3,1,0:T(8,128)(2,1)}), bf16[8,3,128,2,256]{4,2,3,1,0:T(8,128)(2,1)}, u32[]{:S(2)}, u32[]{:S(2)}) async-start(bf16[8,3,128,2,256]{4,2,3,1,0:T(8,128)(2,1)} %bitcast.103), calls=%async_computation.1 | async-start | bytes 6291456 | tf_op jit(solution)/shard_map/all_to_all | solution.py:102
  46.4 59.3 %all-to-all-done.1 = bf16[8,3,128,2,256]{4,2,3,1,0:T(8,128)(2,1)} async-done(((bf16[8,3,128,2,256]{4,2,3,1,0:T(8,128)(2,1)}), bf16[8,3,128,2,256]{4,2,3,1,0:T(8,128)(2,1)}, u32[]{:S(2)}, u32[]{:S(2)}) %all-to-all-start.1) | async-done | bytes 3145760 | tf_op jit(solution)/shard_map/all_to_all | solution.py:102
  105.7 177.6 %while.14 = (s32[]{:T(128)}, f32[2,32,2,8]{0,3,2,1:T(8,128)}, f32[2,32,2,8]{0,3,2,1:T(8,128)}, f32[2,32,2,8,128]{4,0,3,2,1:T(2,128)}, s32[8,3]{1,0:T(8,128)S(1)}...) while((s32[]{:T(128)}, f32[2,32,2,8]{0,3,2,1:T(8,128)}, ...), condition=%wide.region_10.11_spmd, body=%wide.region_6.10_spmd.sunk | while | flops 108984720 | bytes 16320567 | solution.py:108
  105.8 2.3 convolution_convert_fusion.3
  116.4 5.0 %fusion.68 = f32[32,2,8,1,2]{4,3,2,1,0:T(1,128)S(1)} fusion(f32[3,32,2,8,1]{0,4,3,2,1:T(1,128)} %copy.146, pred[3,2]{0,1:T(4,128)(4,1)S(1)} %fusion.67, f32[2,32,2,8]{0,3,2,1:T(8,128)S(1)} %select_reduce_fusion.9, f32[3,32,2,8]{0,3,2,1:T(8,128)S(1)} %copy.147), kind=kOutput, calls=%fused_computation.17.clone.1 | convolution fusion | flops 46080 | bytes 20486 | tf_op jit(solution)/shard_map/while/body/eval_jaxpr/sdnkg,snkg->dnkg/dot_general | solution.py:61
  121.7 5.4 %fusion.69 = f32[2,32,2,8,128]{4,0,3,2,1:T(2,128)S(1)} fusion(f32[3,32,2,8,128]{4,1,3,2,0:T(8,128)S(1)} %copy-done.1, f32[2,32,2,8,128]{4,0,3,2,1:T(2,128)S(1)} %copy-done.6, pred[3,2]{0,1:T(4,128)(4,1)S(1)} %fusion.67, f32[2,32,2,8]{0,3,2,1:T(8,128)S(1)} %get-tuple-element.202, f32[2,32,2,8]{0,3,2,1:T(8,128)S(1)} %get-tuple-element.203, ...), kind=kOutput, calls=%fused_computation.7.clone.1 | convolution fusion | flops 5121024 | bytes 1853446 | tf_op jit(solution)/shard_map/while/body/eval_jaxpr/sdnkg,snkgh->dnkgh/dot_general | solution.py:62
  128.0 2.3 convolution_convert_fusion.3
  138.6 5.0 %fusion.68 = f32[32,2,8,1,2]{4,3,2,1,0:T(1,128)S(1)} fusion(f32[3,32,2,8,1]{0,4,3,2,1:T(1,128)} %copy.146, pred[3,2]{0,1:T(4,128)(4,1)S(1)} %fusion.67, f32[2,32,2,8]{0,3,2,1:T(8,128)S(1)} %select_reduce_fusion.9, f32[3,32,2,8]{0,3,2,1:T(8,128)S(1)} %copy.147), kind=kOutput, calls=%fused_computation.17.clone.1 | convolution fusion | flops 46080 | bytes 20486 | tf_op jit(solution)/shard_map/while/body/eval_jaxpr/sdnkg,snkg->dnkg/dot_general | solution.py:61
  143.9 5.4 %fusion.69 = f32[2,32,2,8,128]{4,0,3,2,1:T(2,128)S(1)} fusion(f32[3,32,2,8,128]{4,1,3,2,0:T(8,128)S(1)} %copy-done.1, f32[2,32,2,8,128]{4,0,3,2,1:T(2,128)S(1)} %copy-done.6, pred[3,2]{0,1:T(4,128)(4,1)S(1)} %fusion.67, f32[2,32,2,8]{0,3,2,1:T(8,128)S(1)} %get-tuple-element.202, f32[2,32,2,8]{0,3,2,1:T(8,128)S(1)} %get-tuple-element.203, ...), kind=kOutput, calls=%fused_computation.7.clone.1 | convolution fusion | flops 5121024 | bytes 1853446 | tf_op jit(solution)/shard_map/while/body/eval_jaxpr/sdnkg,snkgh->dnkgh/dot_general | solution.py:62
  150.2 2.3 convolution_convert_fusion.3
  160.8 5.0 %fusion.68 = f32[32,2,8,1,2]{4,3,2,1,0:T(1,128)S(1)} fusion(f32[3,32,2,8,1]{0,4,3,2,1:T(1,128)} %copy.146, pred[3,2]{0,1:T(4,128)(4,1)S(1)} %fusion.67, f32[2,32,2,8]{0,3,2,1:T(8,128)S(1)} %select_reduce_fusion.9, f32[3,32,2,8]{0,3,2,1:T(8,128)S(1)} %copy.147), kind=kOutput, calls=%fused_computation.17.clone.1 | convolution fusion | flops 46080 | bytes 20486 | tf_op jit(solution)/shard_map/while/body/eval_jaxpr/sdnkg,snkg->dnkg/dot_general | solution.py:61
  166.1 5.4 %fusion.69 = f32[2,32,2,8,128]{4,0,3,2,1:T(2,128)S(1)} fusion(f32[3,32,2,8,128]{4,1,3,2,0:T(8,128)S(1)} %copy-done.1, f32[2,32,2,8,128]{4,0,3,2,1:T(2,128)S(1)} %copy-done.6, pred[3,2]{0,1:T(4,128)(4,1)S(1)} %fusion.67, f32[2,32,2,8]{0,3,2,1:T(8,128)S(1)} %get-tuple-element.202, f32[2,32,2,8]{0,3,2,1:T(8,128)S(1)} %get-tuple-element.203, ...), kind=kOutput, calls=%fused_computation.7.clone.1 | convolution fusion | flops 5121024 | bytes 1853446 | tf_op jit(solution)/shard_map/while/body/eval_jaxpr/sdnkg,snkgh->dnkgh/dot_general | solution.py:62
  172.4 2.3 convolution_convert_fusion.3
  183.0 5.0 %fusion.68 = f32[32,2,8,1,2]{4,3,2,1,0:T(1,128)S(1)} fusion(f32[3,32,2,8,1]{0,4,3,2,1:T(1,128)} %copy.146, pred[3,2]{0,1:T(4,128)(4,1)S(1)} %fusion.67, f32[2,32,2,8]{0,3,2,1:T(8,128)S(1)} %select_reduce_fusion.9, f32[3,32,2,8]{0,3,2,1:T(8,128)S(1)} %copy.147), kind=kOutput, calls=%fused_computation.17.clone.1 | convolution fusion | flops 46080 | bytes 20486 | tf_op jit(solution)/shard_map/while/body/eval_jaxpr/sdnkg,snkg->dnkg/dot_general | solution.py:61
  188.3 5.4 %fusion.69 = f32[2,32,2,8,128]{4,0,3,2,1:T(2,128)S(1)} fusion(f32[3,32,2,8,128]{4,1,3,2,0:T(8,128)S(1)} %copy-done.1, f32[2,32,2,8,128]{4,0,3,2,1:T(2,128)S(1)} %copy-done.6, pred[3,2]{0,1:T(4,128)(4,1)S(1)} %fusion.67, f32[2,32,2,8]{0,3,2,1:T(8,128)S(1)} %get-tuple-element.202, f32[2,32,2,8]{0,3,2,1:T(8,128)S(1)} %get-tuple-element.203, ...), kind=kOutput, calls=%fused_computation.7.clone.1 | convolution fusion | flops 5121024 | bytes 1853446 | tf_op jit(solution)/shard_map/while/body/eval_jaxpr/sdnkg,snkgh->dnkgh/dot_general | solution.py:62
  194.6 2.3 convolution_convert_fusion.3
  205.2 5.0 %fusion.68 = f32[32,2,8,1,2]{4,3,2,1,0:T(1,128)S(1)} fusion(f32[3,32,2,8,1]{0,4,3,2,1:T(1,128)} %copy.146, pred[3,2]{0,1:T(4,128)(4,1)S(1)} %fusion.67, f32[2,32,2,8]{0,3,2,1:T(8,128)S(1)} %select_reduce_fusion.9, f32[3,32,2,8]{0,3,2,1:T(8,128)S(1)} %copy.147), kind=kOutput, calls=%fused_computation.17.clone.1 | convolution fusion | flops 46080 | bytes 20486 | tf_op jit(solution)/shard_map/while/body/eval_jaxpr/sdnkg,snkg->dnkg/dot_general | solution.py:61
  210.5 5.4 %fusion.69 = f32[2,32,2,8,128]{4,0,3,2,1:T(2,128)S(1)} fusion(f32[3,32,2,8,128]{4,1,3,2,0:T(8,128)S(1)} %copy-done.1, f32[2,32,2,8,128]{4,0,3,2,1:T(2,128)S(1)} %copy-done.6, pred[3,2]{0,1:T(4,128)(4,1)S(1)} %fusion.67, f32[2,32,2,8]{0,3,2,1:T(8,128)S(1)} %get-tuple-element.202, f32[2,32,2,8]{0,3,2,1:T(8,128)S(1)} %get-tuple-element.203, ...), kind=kOutput, calls=%fused_computation.7.clone.1 | convolution fusion | flops 5121024 | bytes 1853446 | tf_op jit(solution)/shard_map/while/body/eval_jaxpr/sdnkg,snkgh->dnkgh/dot_general | solution.py:62
  216.8 2.3 convolution_convert_fusion.3
  227.4 5.0 %fusion.68 = f32[32,2,8,1,2]{4,3,2,1,0:T(1,128)S(1)} fusion(f32[3,32,2,8,1]{0,4,3,2,1:T(1,128)} %copy.146, pred[3,2]{0,1:T(4,128)(4,1)S(1)} %fusion.67, f32[2,32,2,8]{0,3,2,1:T(8,128)S(1)} %select_reduce_fusion.9, f32[3,32,2,8]{0,3,2,1:T(8,128)S(1)} %copy.147), kind=kOutput, calls=%fused_computation.17.clone.1 | convolution fusion | flops 46080 | bytes 20486 | tf_op jit(solution)/shard_map/while/body/eval_jaxpr/sdnkg,snkg->dnkg/dot_general | solution.py:61
  232.7 5.4 %fusion.69 = f32[2,32,2,8,128]{4,0,3,2,1:T(2,128)S(1)} fusion(f32[3,32,2,8,128]{4,1,3,2,0:T(8,128)S(1)} %copy-done.1, f32[2,32,2,8,128]{4,0,3,2,1:T(2,128)S(1)} %copy-done.6, pred[3,2]{0,1:T(4,128)(4,1)S(1)} %fusion.67, f32[2,32,2,8]{0,3,2,1:T(8,128)S(1)} %get-tuple-element.202, f32[2,32,2,8]{0,3,2,1:T(8,128)S(1)} %get-tuple-element.203, ...), kind=kOutput, calls=%fused_computation.7.clone.1 | convolution fusion | flops 5121024 | bytes 1853446 | tf_op jit(solution)/shard_map/while/body/eval_jaxpr/sdnkg,snkgh->dnkgh/dot_general | solution.py:62
  239.0 2.3 convolution_convert_fusion.3
  249.6 5.0 %fusion.68 = f32[32,2,8,1,2]{4,3,2,1,0:T(1,128)S(1)} fusion(f32[3,32,2,8,1]{0,4,3,2,1:T(1,128)} %copy.146, pred[3,2]{0,1:T(4,128)(4,1)S(1)} %fusion.67, f32[2,32,2,8]{0,3,2,1:T(8,128)S(1)} %select_reduce_fusion.9, f32[3,32,2,8]{0,3,2,1:T(8,128)S(1)} %copy.147), kind=kOutput, calls=%fused_computation.17.clone.1 | convolution fusion | flops 46080 | bytes 20486 | tf_op jit(solution)/shard_map/while/body/eval_jaxpr/sdnkg,snkg->dnkg/dot_general | solution.py:61
  254.9 5.4 %fusion.69 = f32[2,32,2,8,128]{4,0,3,2,1:T(2,128)S(1)} fusion(f32[3,32,2,8,128]{4,1,3,2,0:T(8,128)S(1)} %copy-done.1, f32[2,32,2,8,128]{4,0,3,2,1:T(2,128)S(1)} %copy-done.6, pred[3,2]{0,1:T(4,128)(4,1)S(1)} %fusion.67, f32[2,32,2,8]{0,3,2,1:T(8,128)S(1)} %get-tuple-element.202, f32[2,32,2,8]{0,3,2,1:T(8,128)S(1)} %get-tuple-element.203, ...), kind=kOutput, calls=%fused_computation.7.clone.1 | convolution fusion | flops 5121024 | bytes 1853446 | tf_op jit(solution)/shard_map/while/body/eval_jaxpr/sdnkg,snkgh->dnkgh/dot_general | solution.py:62
  261.2 2.3 convolution_convert_fusion.3
  271.8 5.0 %fusion.68 = f32[32,2,8,1,2]{4,3,2,1,0:T(1,128)S(1)} fusion(f32[3,32,2,8,1]{0,4,3,2,1:T(1,128)} %copy.146, pred[3,2]{0,1:T(4,128)(4,1)S(1)} %fusion.67, f32[2,32,2,8]{0,3,2,1:T(8,128)S(1)} %select_reduce_fusion.9, f32[3,32,2,8]{0,3,2,1:T(8,128)S(1)} %copy.147), kind=kOutput, calls=%fused_computation.17.clone.1 | convolution fusion | flops 46080 | bytes 20486 | tf_op jit(solution)/shard_map/while/body/eval_jaxpr/sdnkg,snkg->dnkg/dot_general | solution.py:61
  277.0 5.4 %fusion.69 = f32[2,32,2,8,128]{4,0,3,2,1:T(2,128)S(1)} fusion(f32[3,32,2,8,128]{4,1,3,2,0:T(8,128)S(1)} %copy-done.1, f32[2,32,2,8,128]{4,0,3,2,1:T(2,128)S(1)} %copy-done.6, pred[3,2]{0,1:T(4,128)(4,1)S(1)} %fusion.67, f32[2,32,2,8]{0,3,2,1:T(8,128)S(1)} %get-tuple-element.202, f32[2,32,2,8]{0,3,2,1:T(8,128)S(1)} %get-tuple-element.203, ...), kind=kOutput, calls=%fused_computation.7.clone.1 | convolution fusion | flops 5121024 | bytes 1853446 | tf_op jit(solution)/shard_map/while/body/eval_jaxpr/sdnkg,snkgh->dnkgh/dot_general | solution.py:62
  286.8 14.7 %convolution_convert_fusion.1 = bf16[64,8192]{1,0:T(8,128)(2,1)} fusion(bf16[64,2048]{1,0:T(8,128)(2,1)S(1)} %reshape.200, bf16[2048,8192]{1,0:T(8,128)(2,1)} %param.13), kind=kOutput, calls=%fused_computation.45 | convolution fusion | flops 2148007936 | bytes 34865152 | tf_op jit(solution)/shard_map/dot_general | solution.py:115
  301.5 24.6 %reduce-scatter.2.cloned.1.call-done = bf16[16,8192]{1,0:T(8,128)(2,1)} async-done(((bf16[64,8192]{1,0:T(8,128)(2,1)}), bf16[16,8192]{1,0:T(8,128)(2,1)}) %reduce-scatter.2.cloned.1.call-update) | async-done | bytes 262160 | tf_op jit(solution)/shard_map/reduce_scatter | solution.py:114
  (300 shorter events, 91.1 us)
Async XLA Ops:
  6.5 9.5 %copy-start = (bf16[24,128,2,256]{3,2,1,0:T(2,128)(2,1)S(1)}, bf16[24,128,2,256]{3,2,1,0:T(2,128)(2,1)}, u32[]{:S(2)}) copy-start(bf16[24,128,2,256]{3,2,1,0:T(2,128)(2,1)} %param.10) | copy-start | bytes 9437188
  28.2 9.5 %copy-start.8 = (bf16[64,2,256]{2,1,0:T(2,128)(2,1)S(1)}, bf16[64,2,256]{2,1,0:T(2,128)(2,1)}, u32[]{:S(2)}) copy-start(bf16[64,2,256]{2,1,0:T(2,128)(2,1)} %param.9) | copy-start | bytes 196612
  28.2 77.5 %all-to-all-start.1 = ((bf16[8,3,128,2,256]{4,2,3,1,0:T(8,128)(2,1)}), bf16[8,3,128,2,256]{4,2,3,1,0:T(8,128)(2,1)}, u32[]{:S(2)}, u32[]{:S(2)}) async-start(bf16[8,3,128,2,256]{4,2,3,1,0:T(8,128)(2,1)} %bitcast.103), calls=%async_computation.1 | async-start | bytes 6291456 | tf_op jit(solution)/shard_map/all_to_all | solution.py:102
  36.6 289.5 %reduce-scatter.2.cloned.1.call-start = ((), (), s32[]{:S(2)}) async-start(), calls=%async_computation.3 | async-start | bytes 1310720 | tf_op jit(solution)/shard_map/reduce_scatter | solution.py:114
  115.7 5.7 %copy-start.2 = (f32[2,32,2,8]{0,3,2,1:T(8,128)S(1)}, f32[2,32,2,8]{0,3,2,1:T(8,128)}, u32[]{:S(2)}) copy-start(f32[2,32,2,8]{0,3,2,1:T(8,128)} %get-tuple-element.215) | copy-start | bytes 12292 | tf_op jit(solution)/shard_map/while
  115.7 5.7 %copy-start.4 = (f32[2,32,2,8]{0,3,2,1:T(8,128)S(1)}, f32[2,32,2,8]{0,3,2,1:T(8,128)}, u32[]{:S(2)}) copy-start(f32[2,32,2,8]{0,3,2,1:T(8,128)} %get-tuple-element.214) | copy-start | bytes 12292 | tf_op jit(solution)/shard_map/while
  121.6 5.4 %copy-start.3 = (f32[2,32,2,8]{0,3,2,1:T(8,128)}, f32[2,32,2,8]{0,3,2,1:T(8,128)S(1)}, u32[]{:S(2)}) copy-start(f32[2,32,2,8]{0,3,2,1:T(8,128)S(1)} %get-tuple-element.224) | copy-start | bytes 12292 | tf_op jit(solution)/shard_map/while
  121.7 5.4 %copy-start.5 = (f32[2,32,2,8]{0,3,2,1:T(8,128)}, f32[2,32,2,8]{0,3,2,1:T(8,128)S(1)}, u32[]{:S(2)}) copy-start(f32[2,32,2,8]{0,3,2,1:T(8,128)S(1)} %get-tuple-element.223) | copy-start | bytes 12292 | tf_op jit(solution)/shard_map/while
  137.9 5.7 %copy-start.2 = (f32[2,32,2,8]{0,3,2,1:T(8,128)S(1)}, f32[2,32,2,8]{0,3,2,1:T(8,128)}, u32[]{:S(2)}) copy-start(f32[2,32,2,8]{0,3,2,1:T(8,128)} %get-tuple-element.215) | copy-start | bytes 12292 | tf_op jit(solution)/shard_map/while
  137.9 5.7 %copy-start.4 = (f32[2,32,2,8]{0,3,2,1:T(8,128)S(1)}, f32[2,32,2,8]{0,3,2,1:T(8,128)}, u32[]{:S(2)}) copy-start(f32[2,32,2,8]{0,3,2,1:T(8,128)} %get-tuple-element.214) | copy-start | bytes 12292 | tf_op jit(solution)/shard_map/while
  143.8 5.4 %copy-start.3 = (f32[2,32,2,8]{0,3,2,1:T(8,128)}, f32[2,32,2,8]{0,3,2,1:T(8,128)S(1)}, u32[]{:S(2)}) copy-start(f32[2,32,2,8]{0,3,2,1:T(8,128)S(1)} %get-tuple-element.224) | copy-start | bytes 12292 | tf_op jit(solution)/shard_map/while
  143.9 5.4 %copy-start.5 = (f32[2,32,2,8]{0,3,2,1:T(8,128)}, f32[2,32,2,8]{0,3,2,1:T(8,128)S(1)}, u32[]{:S(2)}) copy-start(f32[2,32,2,8]{0,3,2,1:T(8,128)S(1)} %get-tuple-element.223) | copy-start | bytes 12292 | tf_op jit(solution)/shard_map/while
  160.1 5.7 %copy-start.2 = (f32[2,32,2,8]{0,3,2,1:T(8,128)S(1)}, f32[2,32,2,8]{0,3,2,1:T(8,128)}, u32[]{:S(2)}) copy-start(f32[2,32,2,8]{0,3,2,1:T(8,128)} %get-tuple-element.215) | copy-start | bytes 12292 | tf_op jit(solution)/shard_map/while
  160.1 5.7 %copy-start.4 = (f32[2,32,2,8]{0,3,2,1:T(8,128)S(1)}, f32[2,32,2,8]{0,3,2,1:T(8,128)}, u32[]{:S(2)}) copy-start(f32[2,32,2,8]{0,3,2,1:T(8,128)} %get-tuple-element.214) | copy-start | bytes 12292 | tf_op jit(solution)/shard_map/while
  166.0 5.4 %copy-start.3 = (f32[2,32,2,8]{0,3,2,1:T(8,128)}, f32[2,32,2,8]{0,3,2,1:T(8,128)S(1)}, u32[]{:S(2)}) copy-start(f32[2,32,2,8]{0,3,2,1:T(8,128)S(1)} %get-tuple-element.224) | copy-start | bytes 12292 | tf_op jit(solution)/shard_map/while
  166.0 5.4 %copy-start.5 = (f32[2,32,2,8]{0,3,2,1:T(8,128)}, f32[2,32,2,8]{0,3,2,1:T(8,128)S(1)}, u32[]{:S(2)}) copy-start(f32[2,32,2,8]{0,3,2,1:T(8,128)S(1)} %get-tuple-element.223) | copy-start | bytes 12292 | tf_op jit(solution)/shard_map/while
  182.3 5.7 %copy-start.2 = (f32[2,32,2,8]{0,3,2,1:T(8,128)S(1)}, f32[2,32,2,8]{0,3,2,1:T(8,128)}, u32[]{:S(2)}) copy-start(f32[2,32,2,8]{0,3,2,1:T(8,128)} %get-tuple-element.215) | copy-start | bytes 12292 | tf_op jit(solution)/shard_map/while
  182.3 5.7 %copy-start.4 = (f32[2,32,2,8]{0,3,2,1:T(8,128)S(1)}, f32[2,32,2,8]{0,3,2,1:T(8,128)}, u32[]{:S(2)}) copy-start(f32[2,32,2,8]{0,3,2,1:T(8,128)} %get-tuple-element.214) | copy-start | bytes 12292 | tf_op jit(solution)/shard_map/while
  204.5 5.7 %copy-start.2 = (f32[2,32,2,8]{0,3,2,1:T(8,128)S(1)}, f32[2,32,2,8]{0,3,2,1:T(8,128)}, u32[]{:S(2)}) copy-start(f32[2,32,2,8]{0,3,2,1:T(8,128)} %get-tuple-element.215) | copy-start | bytes 12292 | tf_op jit(solution)/shard_map/while
  204.5 5.7 %copy-start.4 = (f32[2,32,2,8]{0,3,2,1:T(8,128)S(1)}, f32[2,32,2,8]{0,3,2,1:T(8,128)}, u32[]{:S(2)}) copy-start(f32[2,32,2,8]{0,3,2,1:T(8,128)} %get-tuple-element.214) | copy-start | bytes 12292 | tf_op jit(solution)/shard_map/while
  210.4 5.4 %copy-start.3 = (f32[2,32,2,8]{0,3,2,1:T(8,128)}, f32[2,32,2,8]{0,3,2,1:T(8,128)S(1)}, u32[]{:S(2)}) copy-start(f32[2,32,2,8]{0,3,2,1:T(8,128)S(1)} %get-tuple-element.224) | copy-start | bytes 12292 | tf_op jit(solution)/shard_map/while
  210.4 5.4 %copy-start.5 = (f32[2,32,2,8]{0,3,2,1:T(8,128)}, f32[2,32,2,8]{0,3,2,1:T(8,128)S(1)}, u32[]{:S(2)}) copy-start(f32[2,32,2,8]{0,3,2,1:T(8,128)S(1)} %get-tuple-element.223) | copy-start | bytes 12292 | tf_op jit(solution)/shard_map/while
  226.7 5.7 %copy-start.2 = (f32[2,32,2,8]{0,3,2,1:T(8,128)S(1)}, f32[2,32,2,8]{0,3,2,1:T(8,128)}, u32[]{:S(2)}) copy-start(f32[2,32,2,8]{0,3,2,1:T(8,128)} %get-tuple-element.215) | copy-start | bytes 12292 | tf_op jit(solution)/shard_map/while
  226.7 5.7 %copy-start.4 = (f32[2,32,2,8]{0,3,2,1:T(8,128)S(1)}, f32[2,32,2,8]{0,3,2,1:T(8,128)}, u32[]{:S(2)}) copy-start(f32[2,32,2,8]{0,3,2,1:T(8,128)} %get-tuple-element.214) | copy-start | bytes 12292 | tf_op jit(solution)/shard_map/while
  232.6 5.4 %copy-start.3 = (f32[2,32,2,8]{0,3,2,1:T(8,128)}, f32[2,32,2,8]{0,3,2,1:T(8,128)S(1)}, u32[]{:S(2)}) copy-start(f32[2,32,2,8]{0,3,2,1:T(8,128)S(1)} %get-tuple-element.224) | copy-start | bytes 12292 | tf_op jit(solution)/shard_map/while
  232.6 5.4 %copy-start.5 = (f32[2,32,2,8]{0,3,2,1:T(8,128)}, f32[2,32,2,8]{0,3,2,1:T(8,128)S(1)}, u32[]{:S(2)}) copy-start(f32[2,32,2,8]{0,3,2,1:T(8,128)S(1)} %get-tuple-element.223) | copy-start | bytes 12292 | tf_op jit(solution)/shard_map/while
  248.9 5.7 %copy-start.2 = (f32[2,32,2,8]{0,3,2,1:T(8,128)S(1)}, f32[2,32,2,8]{0,3,2,1:T(8,128)}, u32[]{:S(2)}) copy-start(f32[2,32,2,8]{0,3,2,1:T(8,128)} %get-tuple-element.215) | copy-start | bytes 12292 | tf_op jit(solution)/shard_map/while
  248.9 5.7 %copy-start.4 = (f32[2,32,2,8]{0,3,2,1:T(8,128)S(1)}, f32[2,32,2,8]{0,3,2,1:T(8,128)}, u32[]{:S(2)}) copy-start(f32[2,32,2,8]{0,3,2,1:T(8,128)} %get-tuple-element.214) | copy-start | bytes 12292 | tf_op jit(solution)/shard_map/while
  254.8 5.4 %copy-start.3 = (f32[2,32,2,8]{0,3,2,1:T(8,128)}, f32[2,32,2,8]{0,3,2,1:T(8,128)S(1)}, u32[]{:S(2)}) copy-start(f32[2,32,2,8]{0,3,2,1:T(8,128)S(1)} %get-tuple-element.224) | copy-start | bytes 12292 | tf_op jit(solution)/shard_map/while
  254.8 5.4 %copy-start.5 = (f32[2,32,2,8]{0,3,2,1:T(8,128)}, f32[2,32,2,8]{0,3,2,1:T(8,128)S(1)}, u32[]{:S(2)}) copy-start(f32[2,32,2,8]{0,3,2,1:T(8,128)S(1)} %get-tuple-element.223) | copy-start | bytes 12292 | tf_op jit(solution)/shard_map/while
  271.1 5.7 %copy-start.2 = (f32[2,32,2,8]{0,3,2,1:T(8,128)S(1)}, f32[2,32,2,8]{0,3,2,1:T(8,128)}, u32[]{:S(2)}) copy-start(f32[2,32,2,8]{0,3,2,1:T(8,128)} %get-tuple-element.215) | copy-start | bytes 12292 | tf_op jit(solution)/shard_map/while
  271.1 5.7 %copy-start.4 = (f32[2,32,2,8]{0,3,2,1:T(8,128)S(1)}, f32[2,32,2,8]{0,3,2,1:T(8,128)}, u32[]{:S(2)}) copy-start(f32[2,32,2,8]{0,3,2,1:T(8,128)} %get-tuple-element.214) | copy-start | bytes 12292 | tf_op jit(solution)/shard_map/while
  (44 other events, 168.1 us)
Sparse Core Ops, SparseCore 0:
  301.6 24.4 reduce-scatter.1
where the time goes:
time: 338 us; the launch traced here: 333 us
  matrix products  142 us (42%)
  waiting for transfers between devices  83.9 us (25%)
  local copies, waits for them, and re-layouts  60.4 us (18%)
  other arithmetic  16.4 us (5%)
  between operations  13.5 us (4%)
  starting transfers between devices  8.35 us (2%)
  blocking collectives  6.71 us (2%)
    all_to_all x1, waiting for transfers between devices, local(): lax.all_to_all(outgoing, 'replica', split_axis=0, concat_axis=0, tiled=True)  59.3 us
    dot_general x8, matrix products, block_stats(): jnp.einsum('sdnkg,snkgh->dnkgh', factor, summed, precision=lax.Precision....  43.1 us
    dot_general x8, matrix products, block_stats(): jnp.einsum('sdnkg,snkg->dnkg', factor, amount, precision=lax.Precision.HI...  39.9 us
    reduce_scatter x1, waiting for transfers between devices, local(): lax.psum_scatter(jnp.dot(attended, o_weight, preferred_element_type=jnp.f...  24.6 us
    dynamic_slice x16, local copies, waits for them, and re-layouts, local(): state, _ = lax.scan(absorb_pages, state, (arrived, dialog_ids, slot_fill))  23.8 us
    dot_general x8, matrix products, block_stats(): jnp.einsum('sd,dnkgh->snkgh', picker, asked, preferred_element_type=jnp.f...  18.1 us
    dot_general x9, matrix products, attend_part(): jnp.einsum('bnkgd,btkd->bnkgt', asked, keys, preferred_element_type=jnp.f...  15 us
    dot_general x1, matrix products, local(): jnp.dot(attended, o_weight, preferred_element_type=jnp.float32)  14.7 us
  transfers between devices with their start and end apart: 2, of which 2 were waited for; matrix products, arithmetic and copies ran while one was open for 3% of the time, Pallas kernels for 0%

commit v1 on v0

v1 whole, which is shorter than its diff:
```python
import functools
import math

import jax
import jax.numpy as jnp
from jax import lax
from jax.experimental import pallas as pl
from jax.experimental.pallas import tpu as pltpu
from jax.sharding import PartitionSpec as P

HD = 128
PAGE = 128
SLOT = 3
TILE = 1024


floor_value = -1e30

MESH = pl.DeviceIdType.MESH


def kernel(
    groups, shards, new_len,
    dialog_ref, fill_ref, q_ref, fresh_ref, outgoing, weight,
    out_ref,
    arrived, wbuf, perm, qs, kbuf, vbuf, peak_ref, amount_ref, summed_ref, attended, part, landed,
    send_sem, recv_sem, own_sem, weight_sem, part_send, part_recv,
):
    me = lax.axis_index("replica")
    mine = lax.axis_index("tensor")
    token_rows = q_ref.shape[0]
    kv_count, rows, _ = qs.shape
    per_group = rows // token_rows
    slots = arrived.shape[1]
    tiles, _, block_rows, tile = part.shape
    scale = 1.0 / math.sqrt(HD)

    own = pltpu.make_async_copy(outgoing.at[me], arrived.at[0], own_sem)
    own.start()

    barrier = pltpu.get_barrier_semaphore()
    for step in range(1, groups):
        pl.semaphore_signal(
            barrier, inc=1, device_id={"replica": lax.rem(me + step, groups)}, device_id_type=MESH
        )
    for step in range(1, shards):
        pl.semaphore_signal(
            barrier, inc=1, device_id={"tensor": lax.rem(mine + step, shards)}, device_id_type=MESH
        )
    pl.semaphore_wait(barrier, groups + shards - 2)

    def page_copy(step):
        dest = lax.rem(me + step, groups)
        return pltpu.make_async_remote_copy(
            src_ref=outgoing.at[dest],
            dst_ref=arrived.at[step],
            send_sem=send_sem.at[step],
            recv_sem=recv_sem.at[step],
            device_id={"replica": dest},
            device_id_type=MESH,
        )

    def weight_copy(index):
        return pltpu.make_async_copy(
            weight.at[:, pl.ds(pl.multiple_of(index * tile, tile), tile)],
            wbuf.at[index],
            weight_sem.at[index],
        )

    def part_copy(index, step):
        dest = lax.rem(mine + step, shards)
        return pltpu.make_async_remote_copy(
            src_ref=part.at[index, dest],
            dst_ref=landed.at[index, step - 1],
            send_sem=part_send.at[index, step - 1],
            recv_sem=part_recv.at[index, step - 1],
            device_id={"tensor": dest},
            device_id_type=MESH,
        )

    for step in range(1, groups):
        page_copy(step).start()
    for index in range(tiles):
        weight_copy(index).start()

    width = perm.shape[0]
    i = lax.broadcasted_iota(jnp.int32, (width, width), 0)
    j = lax.broadcasted_iota(jnp.int32, (width, width), 1)
    source = jnp.where(i < PAGE, 2 * i, 2 * (i - PAGE) + 1)
    perm[...] = jnp.where(source == j, 1.0, 0.0).astype(perm.dtype)

    for k in range(kv_count):
        for g in range(per_group):
            col = (k * per_group + g) * HD
            qs[k, g * token_rows : (g + 1) * token_rows, :] = q_ref[:, col : col + HD]

    contract = (((1,), (1,)), ((), ()))

    row_token = lax.broadcasted_iota(jnp.int32, (rows, token_rows), 0) % token_rows
    col_token = lax.broadcasted_iota(jnp.int32, (rows, token_rows), 1)
    causal = (row_token // new_len == col_token // new_len) & (col_token <= row_token)
    for k in range(kv_count):
        keys = fresh_ref[0, :, k * HD : (k + 1) * HD]
        values = fresh_ref[1, :, k * HD : (k + 1) * HD]
        scores = lax.dot_general(qs[k], keys, contract, preferred_element_type=jnp.float32) * scale
        scores = jnp.where(causal, scores, floor_value)
        peak = jnp.max(scores, axis=-1, keepdims=True)
        weights = jnp.exp(scores - peak).astype(jnp.bfloat16)
        peak_ref[k] = jnp.broadcast_to(peak, (rows, HD))
        amount_ref[k] = jnp.broadcast_to(
            jnp.sum(weights.astype(jnp.float32), axis=-1, keepdims=True), (rows, HD)
        )
        summed_ref[k] = jnp.dot(weights, values, preferred_element_type=jnp.float32)

    def absorb(step):
        owner = lax.rem(me - step + groups, groups)
        row_dialog = (
            lax.broadcasted_iota(jnp.int32, (rows, PAGE), 0) % token_rows
        ) // new_len
        position = lax.broadcasted_iota(jnp.int32, (rows, PAGE), 1)
        allowed = []
        for s in range(slots):
            split = jnp.dot(perm[...], arrived[step, s], preferred_element_type=jnp.float32)
            split = split.astype(jnp.bfloat16)
            kbuf[s * PAGE : (s + 1) * PAGE, :] = split[:PAGE]
            vbuf[s * PAGE : (s + 1) * PAGE, :] = split[PAGE:]
            limit = jnp.where(row_dialog == dialog_ref[owner, s], fill_ref[owner, s], 0)
            allowed.append(position < limit)
        for k in range(kv_count):
            keys = kbuf[:, k * HD : (k + 1) * HD]
            values = vbuf[:, k * HD : (k + 1) * HD]
            scores = (
                lax.dot_general(qs[k], keys, contract, preferred_element_type=jnp.float32) * scale
            )
            pieces = [
                jnp.where(allowed[s], scores[:, s * PAGE : (s + 1) * PAGE], floor_value)
                for s in range(slots)
            ]
            high = functools.reduce(jnp.maximum, pieces)
            before = peak_ref[k]
            peak = jnp.maximum(before, jnp.max(high, axis=-1, keepdims=True))
            keep = jnp.exp(before - peak)
            weights = [jnp.exp(piece - peak).astype(jnp.bfloat16) for piece in pieces]
            added = functools.reduce(jnp.add, [w.astype(jnp.float32) for w in weights])
            peak_ref[k] = peak
            amount_ref[k] = keep * amount_ref[k] + jnp.sum(added, axis=-1, keepdims=True)
            summed_ref[k] = keep * summed_ref[k] + jnp.dot(
                jnp.concatenate(weights, axis=1), values, preferred_element_type=jnp.float32
            )

    own.wait()
    absorb(0)

    def page_step(step, carry):
        page_copy(step).wait_recv()
        absorb(step)
        return carry

    lax.fori_loop(1, groups, page_step, 0)

    for k in range(kv_count):
        for g in range(per_group):
            span = slice(g * token_rows, (g + 1) * token_rows)
            col = (k * per_group + g) * HD
            attended[:, col : col + HD] = (summed_ref[k, span] / amount_ref[k, span]).astype(
                jnp.bfloat16
            )

    def project(index, carry):
        weight_copy(index).wait()
        product = jnp.dot(attended[...], wbuf[index], preferred_element_type=jnp.float32)
        part[index] = product.astype(jnp.bfloat16).reshape(shards, block_rows, tile)
        for step in range(1, shards):
            part_copy(index, step).start()
        return carry

    lax.fori_loop(0, tiles, project, 0)

    def finish(index, carry):
        total = part[index, mine].astype(jnp.float32)
        for step in range(1, shards):
            part_copy(index, step).wait_recv()
            total = total + landed[index, step - 1].astype(jnp.float32)
        out_ref[:, pl.ds(pl.multiple_of(index * tile, tile), tile)] = total.astype(out_ref.dtype)
        return carry

    lax.fori_loop(0, tiles, finish, 0)

    def drain(index, carry):
        for step in range(1, shards):
            part_copy(index, step).wait_send()
        return carry

    lax.fori_loop(0, tiles, drain, 0)
    for step in range(1, groups):
        page_copy(step).wait_send()


def request_lists(page_table, hist_len, groups, pool_size):
    dialogs, entries = page_table.shape
    position = jnp.arange(entries, dtype=jnp.int32)
    fills = jnp.clip(hist_len[:, None] - position[None, :] * PAGE, 0, PAGE).reshape(-1)
    owners = (page_table // pool_size).reshape(-1)
    shelf = (page_table % pool_size).reshape(-1)
    dialog_of = jnp.repeat(jnp.arange(dialogs, dtype=jnp.int32), entries)
    hits = (owners[:, None] == jnp.arange(groups, dtype=jnp.int32)[None, :]) & (fills > 0)[:, None]
    ranks = jnp.cumsum(hits.astype(jnp.int32), axis=0) - 1
    places = hits.T[:, None, :] & (
        ranks.T[:, None, :] == jnp.arange(SLOT, dtype=jnp.int32)[None, :, None]
    )
    picked = places.astype(jnp.int32)
    wanted = jnp.sum(picked * shelf[None, None, :], axis=-1)
    dialog_ids = jnp.sum(picked * dialog_of[None, None, :], axis=-1)
    slot_fill = jnp.sum(picked * fills[None, None, :], axis=-1)
    return (wanted, dialog_ids, slot_fill)


def local(queries, kv_new, pool, page_table, hist_len, o_weight):
    groups = lax.axis_size("replica")
    shards = lax.axis_size("tensor")
    pool_size, page_len, _, kv_width = pool.shape
    dialogs = page_table.shape[0]
    token_rows = queries.shape[0]
    new_len = token_rows // dialogs
    kv_count = kv_width // HD
    per_group = queries.shape[1] // kv_width
    rows = per_group * token_rows
    depth, model = o_weight.shape
    tile = min(TILE, model)
    tiles = model // tile
    block_rows = token_rows // shards
    wanted, dialog_ids, slot_fill = request_lists(page_table, hist_len, groups, pool_size)
    shelf_ids = lax.all_to_all(wanted, "replica", split_axis=0, concat_axis=0, tiled=True)
    outgoing = pool[shelf_ids].reshape(groups, SLOT, 2 * page_len, kv_width)
    fresh = jnp.stack([kv_new[:, 0], kv_new[:, 1]])
    vmem = pl.BlockSpec(memory_space=pltpu.VMEM)
    smem = pl.BlockSpec(memory_space=pltpu.SMEM)
    anywhere = pl.BlockSpec(memory_space=pl.ANY)
    return pl.pallas_call(
        functools.partial(kernel, groups, shards, new_len),
        out_shape=jax.ShapeDtypeStruct((block_rows, model), jnp.bfloat16),
        in_specs=[smem, smem, vmem, vmem, anywhere, anywhere],
        out_specs=vmem,
        scratch_shapes=[
            pltpu.VMEM((groups, SLOT, 2 * page_len, kv_width), jnp.bfloat16),
            pltpu.VMEM((tiles, depth, tile), jnp.bfloat16),
            pltpu.VMEM((2 * page_len, 2 * page_len), jnp.bfloat16),
            pltpu.VMEM((kv_count, rows, HD), jnp.bfloat16),
            pltpu.VMEM((SLOT * page_len, kv_width), jnp.bfloat16),
            pltpu.VMEM((SLOT * page_len, kv_width), jnp.bfloat16),
            pltpu.VMEM((kv_count, rows, HD), jnp.float32),
            pltpu.VMEM((kv_count, rows, HD), jnp.float32),
            pltpu.VMEM((kv_count, rows, HD), jnp.float32),
            pltpu.VMEM((token_rows, depth), jnp.bfloat16),
            pltpu.VMEM((tiles, shards, block_rows, tile), jnp.bfloat16),
            pltpu.VMEM((tiles, shards - 1, block_rows, tile), jnp.bfloat16),
            pltpu.SemaphoreType.DMA((groups,)),
            pltpu.SemaphoreType.DMA((groups,)),
            pltpu.SemaphoreType.DMA,
            pltpu.SemaphoreType.DMA((tiles,)),
            pltpu.SemaphoreType.DMA((tiles, shards - 1)),
            pltpu.SemaphoreType.DMA((tiles, shards - 1)),
        ],
        compiler_params=pltpu.CompilerParams(
            collective_id=0, has_side_effects=True, vmem_limit_bytes=60 * 1024 * 1024
        ),
        name="attend",
    )(dialog_ids, slot_fill, queries, fresh, outgoing, o_weight)


def solution(mesh):
    in_specs = (
        P("replica", "tensor"),
        P("replica", None, "tensor"),
        P("replica", None, None, "tensor"),
        P("replica", None),
        P("replica"),
        P("tensor", None),
    )
    out_specs = P(("replica", "tensor"), None)
    return jax.shard_map(local, mesh=mesh, in_specs=in_specs, out_specs=out_specs, check_vma=False)
```

time: 338 us -> 120 us (0.36); the launches traced: 333 us -> 120 us
  matrix products: 142 us -> 0 us
  Pallas kernels: 0 us -> 92.5 us
  waiting for transfers between devices: 83.9 us -> 0.01 us
  local copies, waits for them, and re-layouts: 60.4 us -> 19.2 us
  other arithmetic: 16.4 us -> 2.65 us
  between operations: 13.5 us -> 0.04 us
  blocking collectives: 6.71 us -> 0 us
    dot_general x43 -> x0, matrix products: 142 us -> none  [the longest x8 43.1 us: block_stats(): jnp.einsum('sdnkg,snkgh->dnkgh', factor, summed, precision=lax.Precision....]
    pallas_call x0 -> x1, Pallas kernels: none -> 92.5 us  [local(): pl.pallas_call(functools.partial(kernel, groups, shards, new_len), out_sh...]
    all_to_all x1, waiting for transfers between devices: 59.3 us -> 0.01 us  [local(): lax.all_to_all(wanted, 'replica', split_axis=0, concat_axis=0, tiled=True)]
    reduce_scatter x1 -> x0, waiting for transfers between devices: 24.6 us -> none  [local(): lax.psum_scatter(jnp.dot(attended, o_weight, preferred_element_type=jnp.f...]
    dynamic_slice x16 -> x0, local copies, waits for them, and re-layouts: 23.8 us -> none  [local(): state, _ = lax.scan(absorb_pages, state, (arrived, dialog_ids, slot_fill))]
    while x150 -> x0, local copies, waits for them, and re-layouts: 10.9 us -> none
    all_to_all x1 -> x0, blocking collectives: 6.71 us -> none  [local(): lax.all_to_all(wanted, 'replica', split_axis=0, concat_axis=0, tiled=True)]
    reduce_sum x8 -> x2, local copies, waits for them, and re-layouts: 7.18 us -> 1.34 us  [the longest x1 0.67 us: request_lists(): dialog_ids = jnp.sum(picked * dialog_of[None, None, :], axis=-1)]
  transfers between devices with their start and end apart: 2 -> 1, of which waited for: 2 -> 0; matrix products, arithmetic and copies ran while one was open for 3% -> 3% of each run, Pallas kernels for 0% -> 0%
where the time goes in v1:
time: 120 us
  Pallas kernels  92.5 us (77%)
  local copies, waits for them, and re-layouts  19.2 us (16%)
  starting transfers between devices  5.44 us (5%)
  other arithmetic  2.65 us (2%)
    pallas_call x1, Pallas kernels, local(): pl.pallas_call(functools.partial(kernel, groups, shards, new_len), out_sh...  92.5 us
    gather x1, local copies, waits for them, and re-layouts, local(): outgoing = pool[shelf_ids].reshape(groups, SLOT, 2 * page_len, kv_width)  8.04 us
    reshape x1, local copies, waits for them, and re-layouts, local(): outgoing = pool[shelf_ids].reshape(groups, SLOT, 2 * page_len, kv_width)  5.74 us
    all_to_all x1, starting transfers between devices, local(): lax.all_to_all(wanted, 'replica', split_axis=0, concat_axis=0, tiled=True)  5.44 us
  transfers between devices with their start and end apart: 1, of which 0 were waited for; matrix products, arithmetic and copies ran while one was open for 3% of the time, Pallas kernels for 0%

profile of v1, /device:TPU:31, one launch (start us, length us, event | category | flops | bytes accessed | tf_op | source)
XLA Modules:
  0.0 119.8 jit_solution(17769701281080585441)
XLA Ops:
  0.0 0.0 copy-start
  0.0 0.8 and_select_fusion.1
  0.8 0.1 eq.41
  0.9 0.8 subtract_clamp_fusion
  1.7 0.1 min.12
  1.8 0.1 fusion.1
  1.9 0.1 copy.21
  2.0 0.1 mul.42
  2.1 0.1 mul.37
  2.2 0.3 select_reduce_fusion
  2.4 0.7 copy.24
  3.1 5.4 %all-to-all-start = ((s32[8,1,3]{2,1,0:T(1,128)}), s32[8,1,3]{2,1,0:T(1,128)S(1)}, u32[]{:S(2)}, u32[]{:S(2)}) async-start(s32[8,1,3]{2,1,0:T(1,128)} %copy.24), calls=%async_computation | async-start | bytes 8192 | tf_op jit(solution)/shard_map/all_to_all | solution.py:233
  8.5 1.0 fusion.4
  9.6 0.6 pad_maximum_fusion.fresh_ref
  10.2 0.7 copy.27.dialog_ref
  10.9 0.7 copy.28.fill_ref
  11.6 0.0 all-to-all-done
  11.6 0.1 copy.25
  11.7 0.1 copy.26
  11.7 0.1 reshape.110
  11.8 0.0 copy-done
  11.8 8.0 %gather_fusion = bf16[24,128,2,256]{3,2,1,0:T(2,128)(2,1)} fusion(bf16[24,128,2,256]{3,2,1,0:T(2,128)(2,1)S(1)} %copy-done, s32[1024]{0:T(1024)S(1)} %pad_clamp_fusion), kind=kCustom, calls=%fused_computation | custom fusion | bytes 6291552 | tf_op jit(solution)/shard_map/gather | solution.py:234
  19.9 5.7 %reshape.107.outgoing = bf16[8,3,256,256]{3,2,1,0:T(8,128)(2,1)} reshape(bf16[24,128,2,256]{3,2,1,0:T(2,128)(2,1)} %gather_fusion) | data formatting | bytes 6291456 | tf_op jit(solution)/shard_map/reshape | solution.py:234
  25.6 92.5 %attend.1 = bf16[16,8192]{1,0:T(8,128)(2,1)} custom-call(s32[8,3]{1,0:T(8,128)} %copy.27.dialog_ref, s32[8,3]{1,0:T(8,128)} %copy.28.fill_ref, bf16[64,2048]{1,0:T(8,128)(2,1)} %q_ref.1, bf16[2,64,256]{2,1,0:T(8,128)(2,1)} %pad_maximum_fusion.fresh_ref, bf16[8,3,256,256]{3,2,1,0:T(8,128)(2,1)} %reshape.107.outgoing, bf16[2048,8192]{1,0:T(8,128)(2,1)} %weight.1), custom_call_target="tpu_custom_call" | custom-call | tf_op jit(solution)/shard_map/attend/pallas_call | solution.py:239
  118.1 1.7 %copy.34 = bf16[16,8192]{1,0:T(8,128)(2,1)} copy(bf16[16,8192]{1,0:T(8,128)(2,1)} %attend.1) | data formatting | bytes 524288
  (9 shorter events, 0.1 us)
Async XLA Ops:
  0.0 11.8 %copy-start = (bf16[24,128,2,256]{3,2,1,0:T(2,128)(2,1)S(1)}, bf16[24,128,2,256]{3,2,1,0:T(2,128)(2,1)}, u32[]{:S(2)}) copy-start(bf16[24,128,2,256]{3,2,1,0:T(2,128)(2,1)} %param.8) | copy-start | bytes 9437188
  3.1 8.5 %all-to-all-start = ((s32[8,1,3]{2,1,0:T(1,128)}), s32[8,1,3]{2,1,0:T(1,128)S(1)}, u32[]{:S(2)}, u32[]{:S(2)}) async-start(s32[8,1,3]{2,1,0:T(1,128)} %copy.24), calls=%async_computation | async-start | bytes 8192 | tf_op jit(solution)/shard_map/all_to_all | solution.py:233

commit v2 on v1

--- a/solution.py
+++ b/solution.py
@@ -21,10 +21,10 @@
 
 def kernel(
     groups, shards, new_len,
-    dialog_ref, fill_ref, q_ref, fresh_ref, outgoing, weight,
+    shelf_ref, dialog_ref, fill_ref, q_ref, fresh_ref, pool_ref, weight,
     out_ref,
-    arrived, wbuf, perm, qs, kbuf, vbuf, peak_ref, amount_ref, summed_ref, attended, part, landed,
-    send_sem, recv_sem, own_sem, weight_sem, part_send, part_recv,
+    outgoing, arrived, wbuf, perm, qs, kbuf, vbuf, peak_ref, amount_ref, summed_ref, attended, part, landed,
+    send_sem, recv_sem, weight_sem, part_send, part_recv,
 ):
     me = lax.axis_index("replica")
     mine = lax.axis_index("tensor")
@@ -35,9 +35,6 @@
     tiles, _, block_rows, tile = part.shape
     scale = 1.0 / math.sqrt(HD)
 
-    own = pltpu.make_async_copy(outgoing.at[me], arrived.at[0], own_sem)
-    own.start()
-
     barrier = pltpu.get_barrier_semaphore()
     for step in range(1, groups):
         pl.semaphore_signal(
@@ -47,12 +44,20 @@
         pl.semaphore_signal(
             barrier, inc=1, device_id={"tensor": lax.rem(mine + step, shards)}, device_id_type=MESH
         )
+
+    def collect(step, carry):
+        dest = lax.rem(me + step, groups)
+        for s in range(slots):
+            outgoing[step, s] = pool_ref[shelf_ref[dest, s]]
+        return carry
+
+    lax.fori_loop(0, groups, collect, 0)
     pl.semaphore_wait(barrier, groups + shards - 2)
 
     def page_copy(step):
         dest = lax.rem(me + step, groups)
         return pltpu.make_async_remote_copy(
-            src_ref=outgoing.at[dest],
+            src_ref=outgoing.at[step],
             dst_ref=arrived.at[step],
             send_sem=send_sem.at[step],
             recv_sem=recv_sem.at[step],
@@ -112,7 +117,7 @@
         )
         summed_ref[k] = jnp.dot(weights, values, preferred_element_type=jnp.float32)
 
-    def absorb(step):
+    def absorb(step, pages):
         owner = lax.rem(me - step + groups, groups)
         row_dialog = (
             lax.broadcasted_iota(jnp.int32, (rows, PAGE), 0) % token_rows
@@ -120,7 +125,7 @@
         position = lax.broadcasted_iota(jnp.int32, (rows, PAGE), 1)
         allowed = []
         for s in range(slots):
-            split = jnp.dot(perm[...], arrived[step, s], preferred_element_type=jnp.float32)
+            split = jnp.dot(perm[...], pages[step, s], preferred_element_type=jnp.float32)
             split = split.astype(jnp.bfloat16)
             kbuf[s * PAGE : (s + 1) * PAGE, :] = split[:PAGE]
             vbuf[s * PAGE : (s + 1) * PAGE, :] = split[PAGE:]
@@ -148,12 +153,11 @@
                 jnp.concatenate(weights, axis=1), values, preferred_element_type=jnp.float32
             )
 
-    own.wait()
-    absorb(0)
+    absorb(0, outgoing)
 
     def page_step(step, carry):
         page_copy(step).wait_recv()
-        absorb(step)
+        absorb(step, arrived)
         return carry
 
     lax.fori_loop(1, groups, page_step, 0)
@@ -231,7 +235,7 @@
     block_rows = token_rows // shards
     wanted, dialog_ids, slot_fill = request_lists(page_table, hist_len, groups, pool_size)
     shelf_ids = lax.all_to_all(wanted, "replica", split_axis=0, concat_axis=0, tiled=True)
-    outgoing = pool[shelf_ids].reshape(groups, SLOT, 2 * page_len, kv_width)
+    pages = pool.reshape(pool_size, 2 * page_len, kv_width)
     fresh = jnp.stack([kv_new[:, 0], kv_new[:, 1]])
     vmem = pl.BlockSpec(memory_space=pltpu.VMEM)
     smem = pl.BlockSpec(memory_space=pltpu.SMEM)
@@ -239,9 +243,10 @@
     return pl.pallas_call(
         functools.partial(kernel, groups, shards, new_len),
         out_shape=jax.ShapeDtypeStruct((block_rows, model), jnp.bfloat16),
-        in_specs=[smem, smem, vmem, vmem, anywhere, anywhere],
+        in_specs=[smem, smem, smem, vmem, vmem, vmem, anywhere],
         out_specs=vmem,
         scratch_shapes=[
+            pltpu.VMEM((groups, SLOT, 2 * page_len, kv_width), jnp.bfloat16),
             pltpu.VMEM((groups, SLOT, 2 * page_len, kv_width), jnp.bfloat16),
             pltpu.VMEM((tiles, depth, tile), jnp.bfloat16),
             pltpu.VMEM((2 * page_len, 2 * page_len), jnp.bfloat16),
@@ -256,16 +261,15 @@
             pltpu.VMEM((tiles, shards - 1, block_rows, tile), jnp.bfloat16),
             pltpu.SemaphoreType.DMA((groups,)),
             pltpu.SemaphoreType.DMA((groups,)),
-            pltpu.SemaphoreType.DMA,
             pltpu.SemaphoreType.DMA((tiles,)),
             pltpu.SemaphoreType.DMA((tiles, shards - 1)),
             pltpu.SemaphoreType.DMA((tiles, shards - 1)),
         ],
         compiler_params=pltpu.CompilerParams(
-            collective_id=0, has_side_effects=True, vmem_limit_bytes=60 * 1024 * 1024
+            collective_id=0, has_side_effects=True, vmem_limit_bytes=63 * 1024 * 1024
         ),
         name="attend",
-    )(dialog_ids, slot_fill, queries, fresh, outgoing, o_weight)
+    )(shelf_ids, dialog_ids, slot_fill, queries, fresh, pages, o_weight)
 
 
 def solution(mesh):

time: 120 us -> 112 us (0.933)
  local copies, waits for them, and re-layouts: 19.2 us -> 11.5 us
    gather x1 -> x0, local copies, waits for them, and re-layouts: 8.04 us -> none  [local(): outgoing = pool[shelf_ids].reshape(groups, SLOT, 2 * page_len, kv_width)]
  transfers between devices with their start and end apart: 1 -> 1, of which waited for: 0 -> 0; matrix products, arithmetic and copies ran while one was open for 3% -> 8% of each run, Pallas kernels for 0% -> 0%
where the time goes in v2:
time: 112 us; the launch traced here: 111 us
  Pallas kernels  92 us (82%)
  local copies, waits for them, and re-layouts  11.5 us (10%)
  starting transfers between devices  5.44 us (5%)
  other arithmetic  2.46 us (2%)
    pallas_call x1, Pallas kernels, local(): pl.pallas_call(functools.partial(kernel, groups, shards, new_len), out_sh...  92 us
    reshape x1, local copies, waits for them, and re-layouts, local(): pages = pool.reshape(pool_size, 2 * page_len, kv_width)  5.74 us
    all_to_all x1, starting transfers between devices, local(): lax.all_to_all(wanted, 'replica', split_axis=0, concat_axis=0, tiled=True)  5.44 us
    unnamed x3, local copies, waits for them, and re-layouts  2.26 us
  transfers between devices with their start and end apart: 1, of which 0 were waited for; matrix products, arithmetic and copies ran while one was open for 8% of the time, Pallas kernels for 0%

profile of v2, /device:TPU:31, one launch (start us, length us, event | category | flops | bytes accessed | tf_op | source)
XLA Modules:
  0.0 111.4 jit_solution(5323348528405712627)
XLA Ops:
  0.0 0.7 subtract_clamp_fusion
  0.7 0.1 min.12
  0.8 0.7 and_select_fusion
  1.5 0.1 eq.41
  1.6 0.1 fusion.1
  1.7 0.1 mul.40
  1.8 0.1 mul.37
  1.9 0.1 copy.17
  2.0 0.3 select_reduce_fusion
  2.2 0.7 copy.18
  2.9 5.4 %all-to-all-start = ((s32[8,1,3]{2,1,0:T(1,128)}), s32[8,1,3]{2,1,0:T(1,128)S(1)}, u32[]{:S(2)}, u32[]{:S(2)}) async-start(s32[8,1,3]{2,1,0:T(1,128)} %copy.18), calls=%async_computation | async-start | bytes 8192 | tf_op jit(solution)/shard_map/all_to_all | solution.py:237
  8.4 0.7 copy.24.fill_ref
  9.0 1.0 fusion.4
  10.1 0.6 pad_maximum_fusion.fresh_ref
  10.7 0.7 copy.23.dialog_ref
  11.4 5.7 %reshape.79.pool_ref = bf16[24,256,256]{2,1,0:T(8,128)(2,1)} reshape(bf16[24,128,2,256]{3,2,1,0:T(2,128)(2,1)} %param.8) | data formatting | bytes 6291456 | tf_op jit(solution)/shard_map/reshape | solution.py:238
  17.1 0.0 all-to-all-done
  17.1 0.0 copy-start
  17.1 0.6 copy-done
  17.7 92.0 %attend.1 = bf16[16,8192]{1,0:T(8,128)(2,1)} custom-call(s32[8,3]{1,0:T(8,128)} %bitcast.8, s32[8,3]{1,0:T(8,128)} %copy.23.dialog_ref, s32[8,3]{1,0:T(8,128)} %copy.24.fill_ref, bf16[64,2048]{1,0:T(8,128)(2,1)} %q_ref.1, bf16[2,64,256]{2,1,0:T(8,128)(2,1)} %pad_maximum_fusion.fresh_ref, bf16[24,256,256]{2,1,0:T(8,128)(2,1)} %reshape.79.pool_ref, ...), custom_call_target="tpu_custom_call" | custom-call | tf_op jit(solution)/shard_map/attend/pallas_call | solution.py:243
  109.7 1.7 %copy.31 = bf16[16,8192]{1,0:T(8,128)(2,1)} copy(bf16[16,8192]{1,0:T(8,128)(2,1)} %attend.1) | data formatting | bytes 524288
  (7 shorter events, 0.1 us)
Async XLA Ops:
  2.9 14.2 %all-to-all-start = ((s32[8,1,3]{2,1,0:T(1,128)}), s32[8,1,3]{2,1,0:T(1,128)S(1)}, u32[]{:S(2)}, u32[]{:S(2)}) async-start(s32[8,1,3]{2,1,0:T(1,128)} %copy.18), calls=%async_computation | async-start | bytes 8192 | tf_op jit(solution)/shard_map/all_to_all | solution.py:237
  17.1 0.6 copy-start
